TPU v7x, 256 devices: a whole 4x4x8 slice. The times are simulated.
256 devices in a mesh: section: 8 (over z), ep: 32 (over x, y, core).
Axes of the slice: x: 4, y: 4, z: 8, core: 2. Of those that a mesh axis runs over, the one named last changes fastest.
Arguments:
- saved_inputs: bfloat16 [8, 4096, 4096], P('section', 'ep'), may hold values from -6 to 6
- expert_ids: int32 [8, 4096, 2], P('section', 'ep'), may hold values from 0 to 7, as said below
- gate_weights: float32 [8, 4096, 2], P('section', 'ep'), may hold values from 0.1 to 0.9
- out_grad: bfloat16 [4096, 4096], P('ep', 'section'), may hold values from -6 to 6
- gate_w: bfloat16 [8, 7168, 4096], P('section', 'ep'), may hold values from -0.09375 to 0.09375
- up_w: bfloat16 [8, 7168, 4096], P('section', 'ep'), may hold values from -0.09375 to 0.09375
- down_w: bfloat16 [8, 7168, 4096], P('section', 'ep'), may hold values from -0.0625 to 0.0625
Outputs:
- input_grads: bfloat16 [8, 4096, 4096], P('section', 'ep')
- grad_gate: bfloat16 [8, 7168, 4096], P('section', 'ep')
- grad_up: bfloat16 [8, 7168, 4096], P('section', 'ep')
- grad_down: bfloat16 [8, 7168, 4096], P('section', 'ep')
Inputs may be any that keep to these rules, and one draw needn't show every extreme that they name: `expert_ids`: the two ids of a token differ. Among the 128 tokens of one device in one layer, at most 4 name expert 0, and in every layer some device's tokens name it exactly 4 times.
All inputs are finite; a program needn't handle non-finite values.
Results may differ from a plain program's by a relative error of at most 0.0058.
Values may be sent and summed in bfloat16 or wider, within the bound.
No kernel may reach another device: no remote copies, remote signals or barrier semaphores. Data moves between devices by JAX's collectives and lax.ppermute only.
A program may use at most 128 MiB of HBM per device.

v0:
```python
import jax
import jax.numpy as jnp
from jax import lax
from jax.experimental import pallas as pl
from jax.experimental.pallas import tpu as pltpu
from jax.sharding import PartitionSpec as P


CAP = 4
ROWS = 2 * CAP
FEW = 16
PARTS = 3
LANES = 128
F32 = jnp.float32
BF16 = jnp.bfloat16


def exchange(blocks, axis, groups=None):
    return lax.all_to_all(blocks, axis, 0, 0, tiled=True, axis_index_groups=groups)


def repeated(value, count):
    return jnp.broadcast_to(value[None], (count, *value.shape))


def from_partner(value, devices):
    return lax.ppermute(value, "ep", [(i, i ^ 1) for i in range(devices)])


def project(row_data, weight):
    return lax.dot_general(
        row_data, weight, (((1,), (1,)), ((), ())), preferred_element_type=F32
    )


def matmul(left, right):
    return jnp.dot(left, right, preferred_element_type=F32)


def sum_rows(left, right):
    return lax.dot_general(
        left, right, (((0,), (0,)), ((), ())), preferred_element_type=F32
    )


def iota(shape, dim):
    return lax.broadcasted_iota(jnp.int32, shape, dim)


def grant(mebibytes):
    return pltpu.CompilerParams(vmem_limit_bytes=mebibytes << 20)


def as_float(mask):
    return jnp.where(mask, 1.0, 0.0)


def whole_spec(shape):
    return pl.BlockSpec(shape, lambda: (0,) * len(shape))


def first_pass(where, x_mine, x_other, mine, other, w_gate, w_up, w_down, sections):
    half = mine.shape[0] // ROWS
    rows = half * ROWS
    side = x_mine.shape[1]
    devices = 2 * half
    codes = sections * CAP
    ending = codes + PARTS * CAP
    units, width = w_gate.shape
    columns = width // devices

    def kernel(
        where_ref,
        x_mine_ref,
        x_other_ref,
        mine_ref,
        other_ref,
        w_gate_ref,
        w_up_ref,
        w_down_ref,
        feeds_ref,
        pick_ref,
        weight_ref,
        note_ref,
        column_ref,
        rows_ref,
        scaled_ref,
        act_ref,
        slope_ref,
        hidden_ref,
        gate_ref,
        up_ref,
        act_few_ref,
        slope_few_ref,
        hidden_few_ref,
        gate_few_ref,
        up_few_ref,
        rows_few_ref,
        y_few_ref,
        share_ref,
        fits_ref,
        trips_ref,
    ):
        section = where_ref[0]
        core = where_ref[1]
        place = where_ref[2]

        lead = as_float(iota((half, rows), 1) == ROWS * iota((half, rows), 0)).astype(BF16)
        tiles = [ref[:, side:] for ref in (mine_ref, other_ref)]
        near = matmul(lead, tiles[0])
        far = matmul(lead, tiles[1])
        note = jnp.concatenate([jnp.where(core == 0, near, far), jnp.where(core == 0, far, near)], 0)
        note_ref[...] = note
        lane = iota((devices, LANES), 1)
        code = jnp.where(lane < codes, note, -1.0)
        flag = as_float(code >= 0)
        row = iota((LANES, LANES), 0)
        col = iota((LANES, LANES), 1)
        same_layer = row // CAP == col // CAP
        per_layer = matmul(flag, as_float(same_layer))
        longest = jnp.max(jnp.sum(per_layer, axis=0, keepdims=True))
        fits_ref[0] = (longest <= FEW).astype(jnp.int32)
        most = jnp.max(jnp.where(lane == codes + PARTS * CAP, note, 0.0))
        trips_ref[0] = most.astype(jnp.int32) - 1
        before = as_float(iota((devices, devices), 1) < iota((devices, devices), 0))
        rank = matmul(before, per_layer) + matmul(flag, as_float(same_layer & (row < col)))
        rank = (rank + 1.0) * flag
        token = (code + 1.0) * flag
        owned = as_float(iota((8, LANES), 1) == iota((8, LANES), 0) + CAP * section)
        own_rank = project(owned, rank)
        own_token = project(owned, token)
        entry = iota((FEW, devices), 0).astype(F32) + 1.0
        device = iota((devices, 2 * rows), 0)
        spot = iota((devices, 2 * rows), 1)
        home = rows * ((device // half + core) % 2) + ROWS * (device % half)
        held = jnp.zeros((FEW, 1), F32)
        weight = jnp.zeros((FEW, LANES), F32)
        groups = jnp.zeros((FEW, devices), F32)
        pick = jnp.zeros((FEW, 2 * rows), F32)
        few_lane = iota((FEW, LANES), 1)
        for slot in range(CAP):
            here = as_float(own_rank[slot : slot + 1] == entry)
            groups = groups + here
            held = held + jnp.sum(here * own_token[slot : slot + 1], axis=1, keepdims=True)
            part = matmul(here, note)
            wanted = (few_lane >= codes) & (few_lane < ending) & (few_lane % CAP == slot)
            weight = weight + jnp.where(wanted, part, 0.0)
            pick = pick + matmul(here, as_float(spot == home + slot))
        near_rank = matmul(groups, rank)
        near_token = matmul(groups, token)
        match = (near_token == held) & (near_token > 0) & (few_lane // CAP > section)
        source = jnp.where(match & (few_lane < codes), near_rank, 0.0)
        feeds = jnp.zeros((FEW, LANES), F32)
        for slot in range(CAP):
            spread = as_float((row // CAP == col // FEW) & (row % CAP == slot))
            feeds = feeds + as_float(
                matmul(source, spread) == (few_lane % FEW + 1).astype(F32)
            )
        feeds_ref[...] = feeds.astype(BF16)
        pick_low = pick.astype(BF16)
        pick_ref[...] = pick_low
        weight_ref[...] = jnp.broadcast_to(
            jnp.sum(weight, axis=1, keepdims=True), (FEW, LANES)
        )

        tile_row = iota((rows, LANES), 0)
        tile_lane = iota((rows, LANES), 1)
        wanted = (tile_lane >= codes) & (tile_lane < ending) & (tile_lane % CAP == tile_row % CAP)
        for index, ref in enumerate((mine_ref, other_ref)):
            scale = jnp.sum(
                jnp.where(wanted, tiles[index].astype(F32), 0.0), axis=1, keepdims=True
            )
            part = slice(index * rows, (index + 1) * rows)
            scaled_ref[part, :] = (ref[:, :side].astype(F32) * scale).astype(BF16)
            rows_ref[part, :] = (x_mine_ref, x_other_ref)[index][...]
        y_few_ref[...] = jnp.zeros((FEW, width), BF16)
        blocks = side // columns
        spot = pl.ds(pl.multiple_of(place % blocks * columns, columns), columns)
        column = jnp.concatenate([mine_ref[:, spot], other_ref[:, spot]], 0).astype(F32)
        column = jnp.where(place < blocks, column, pltpu.roll(column, 2 * rows - CAP, 0))
        column_ref[...] = column.astype(BF16)
        rows_few_ref[...] = matmul(pick_low, column_ref[...])
        x_lane = iota((units, 2 * rows), 1) % ROWS < CAP

        def whole_rows(weight_ref, ref):
            return project(weight_ref[:, :side], ref[...]) + pltpu.roll(
                project(weight_ref[:, side:], ref[...]), 2 * rows - CAP, 1
            )

        grad = whole_rows(w_down_ref, scaled_ref)
        gate_pre = whole_rows(w_gate_ref, rows_ref)
        up_pre = whole_rows(w_up_ref, rows_ref)
        sig = 1.0 / (1.0 + jnp.exp(-gate_pre))
        act = jnp.where(x_lane, gate_pre * sig, 0.0)
        slope = jnp.where(x_lane, up_pre * sig * (1.0 + gate_pre * (1.0 - sig)), 0.0)
        act_ref[...] = act
        slope_ref[...] = slope
        hidden_ref[...] = (act * up_pre).astype(BF16)
        gate_ref[...] = (grad * slope).astype(BF16)
        up_ref[...] = (grad * act).astype(BF16)

        def exact(value):
            total = jnp.zeros((units, FEW), F32)
            for _ in range(PARTS):
                piece = value.astype(BF16)
                total = total + project(piece, pick_low)
                value = value - piece.astype(F32)
            return total

        act_few_ref[...] = exact(act_ref[...])
        slope_few_ref[...] = exact(slope_ref[...])
        hidden_few_ref[...] = project(hidden_ref[...], pick_low).astype(BF16)
        gate_few = project(gate_ref[...], pick_low).astype(BF16)
        up_few = project(up_ref[...], pick_low).astype(BF16)
        gate_few_ref[...] = gate_few
        up_few_ref[...] = up_few
        share = (sum_rows(gate_few, w_gate_ref[...]) + sum_rows(up_few, w_up_ref[...])).astype(BF16)
        for index in range(devices):
            share_ref[index] = share[:, index * columns : (index + 1) * columns]

    shapes = [
        ((FEW, sections * FEW), BF16),
        ((FEW, ROWS * devices), BF16),
        ((FEW, LANES), F32),
        ((devices, LANES), F32),
        ((2 * rows, columns), BF16),
        ((2 * rows, side), BF16),
        ((2 * rows, side), BF16),
        ((units, 2 * rows), F32),
        ((units, 2 * rows), F32),
        ((units, 2 * rows), BF16),
        ((units, 2 * rows), BF16),
        ((units, 2 * rows), BF16),
        ((units, FEW), F32),
        ((units, FEW), F32),
        ((units, FEW), BF16),
        ((units, FEW), BF16),
        ((units, FEW), BF16),
        ((FEW, columns), F32),
        ((FEW, width), BF16),
        ((devices, FEW, columns), BF16),
    ]
    smem = pl.BlockSpec(memory_space=pltpu.SMEM)
    return pl.pallas_call(
        kernel,
        compiler_params=grant(28),
        in_specs=[smem] + [whole_spec(value.shape) for value in (x_mine, x_other, mine, other)] + [whole_spec(w_gate.shape)] * 3,
        out_specs=[whole_spec(shape) for shape, _ in shapes] + [smem] * 2,
        out_shape=[jax.ShapeDtypeStruct(shape, dtype) for shape, dtype in shapes]
        + [jax.ShapeDtypeStruct((1,), jnp.int32)] * 2,
    )(where, x_mine, x_other, mine, other, w_gate, w_up, w_down)


def chain_rows(layers, feeds, first_rows, weight, devices):
    sections = layers.shape[0]
    size, columns = first_rows.shape

    def kernel(layers_ref, feeds_ref, first_ref, weight_ref, out_ref):
        rows = first_ref[...]
        for layer in range(sections - 1, 0, -1):
            feed = feeds_ref[:, layer * size : (layer + 1) * size]
            added = matmul(feed, layers_ref[layer, :size, :]) + matmul(
                feed, layers_ref[layer, size:, :]
            )
            rows = (rows + added).astype(BF16).astype(F32)
        rows = (weight_ref[...] * rows).astype(BF16)
        for device in range(devices):
            out_ref[device] = rows

    values = (layers, feeds, first_rows, weight)
    shape = (devices, size, columns)
    return pl.pallas_call(
        kernel,
        compiler_params=grant(8),
        in_specs=[whole_spec(value.shape) for value in values],
        out_specs=whole_spec(shape),
        out_shape=jax.ShapeDtypeStruct(shape, BF16),
    )(*values)


def chain_step(last, y_blocks, act_few, slope_few, w_gate, w_up, w_down):
    devices, size, columns = y_blocks.shape
    units, width = w_gate.shape

    def kernel(
        last_ref,
        blocks_ref,
        act_ref,
        slope_ref,
        w_gate_ref,
        w_up_ref,
        w_down_ref,
        y_ref,
        gate_few_ref,
        up_few_ref,
        share_ref,
    ):
        for index in range(devices):
            y_ref[:, index * columns : (index + 1) * columns] = blocks_ref[index]
        grad = project(w_down_ref[...], y_ref[...])
        gate_few = (grad * slope_ref[...]).astype(BF16)
        up_few = (grad * act_ref[...]).astype(BF16)
        gate_few_ref[...] = gate_few
        up_few_ref[...] = up_few

        @pl.when(last_ref[0] == 0)
        def _():
            share = sum_rows(gate_few, w_gate_ref[...])
            share = (share + sum_rows(up_few, w_up_ref[...])).astype(BF16)
            for index in range(devices):
                share_ref[index] = share[:, index * columns : (index + 1) * columns]

    shapes = [(size, width), (units, size), (units, size), (devices, size, columns)]
    return pl.pallas_call(
        kernel,
        compiler_params=grant(16),
        in_specs=[pl.BlockSpec(memory_space=pltpu.SMEM)]
        + [whole_spec(value.shape) for value in (y_blocks, act_few, slope_few)]
        + [whole_spec(w_gate.shape)] * 3,
        out_specs=[whole_spec(shape) for shape in shapes],
        out_shape=[jax.ShapeDtypeStruct(shape, BF16) for shape in shapes],
    )(last, y_blocks, act_few, slope_few, w_gate, w_up, w_down)


def merge_chains(pick, gate, up, hidden, gate_few, up_few, w_gate, w_up):
    units, width = w_gate.shape
    lanes = gate.shape[1]
    rows = lanes // 2

    def kernel(
        pick_ref,
        gate_ref,
        up_ref,
        hidden_ref,
        gate_few_ref,
        up_few_ref,
        w_gate_ref,
        w_up_ref,
        gate_out,
        up_out,
        hidden_out,
        mine_out,
        other_out,
    ):
        pick_low = pick_ref[...]
        keep = jnp.sum(pick_low.astype(F32), axis=0, keepdims=True) == 0.0
        gate_all = jnp.where(keep, gate_ref[...].astype(F32), matmul(gate_few_ref[...], pick_low))
        up_all = jnp.where(keep, up_ref[...].astype(F32), matmul(up_few_ref[...], pick_low))
        kept = jnp.where(keep, hidden_ref[...].astype(F32), 0.0)
        for ref, value in ((gate_out, gate_all), (up_out, up_all), (hidden_out, kept)):
            ref[0] = value.astype(BF16)
            ref[1] = pltpu.roll(value, CAP, 1).astype(BF16)
        side = width // 2

        def shares(ref, weight_ref):
            return sum_rows(ref[0], weight_ref[:, :side]) + sum_rows(ref[1], weight_ref[:, side:])

        share = (shares(gate_out, w_gate_ref) + shares(up_out, w_up_ref)).astype(BF16)
        mine_out[...] = share[:rows]
        other_out[...] = share[rows:]

    shapes = [(2, units, lanes)] * 3 + [(rows, width // 2)] * 2
    values = (pick, gate, up, hidden, gate_few, up_few)
    return pl.pallas_call(
        kernel,
        compiler_params=grant(16),
        in_specs=[whole_spec(value.shape) for value in values] + [whole_spec(w_gate.shape)] * 2,
        out_specs=[whole_spec(shape) for shape in shapes],
        out_shape=[jax.ShapeDtypeStruct(shape, BF16) for shape in shapes],
    )(*values, w_gate, w_up)


def weight_gradients(x_rows, y_rows, gate, up, hidden, hidden_few, y_few):
    _, units, lanes = gate.shape
    few, width = y_few.shape
    block = 512
    per_side = x_rows.shape[1] // block

    def kernel(x_ref, y_ref, gate_ref, up_ref, h_ref, hf_ref, yf_ref, gate_out, up_out, down_out):
        gate_out[...] = matmul(gate_ref[0], x_ref[...]).astype(BF16)
        up_out[...] = matmul(up_ref[0], x_ref[...]).astype(BF16)
        down_out[...] = (
            matmul(h_ref[0], y_ref[...]) + matmul(hf_ref[...], yf_ref[...])
        ).astype(BF16)

    half = pl.BlockSpec((1, units, lanes), lambda i: (i // per_side, 0, 0))
    side = pl.BlockSpec((lanes, block), lambda i: (0, i % per_side))
    across = lambda count: pl.BlockSpec((count, block), lambda i: (0, i))
    return pl.pallas_call(
        kernel,
        compiler_params=grant(16),
        grid=(width // block,),
        in_specs=[side, side, half, half, half]
        + [pl.BlockSpec(hidden_few.shape, lambda i: (0, 0)), across(few)],
        out_specs=[across(units)] * 3,
        out_shape=[jax.ShapeDtypeStruct((units, width), BF16)] * 3,
    )(x_rows, y_rows, gate, up, hidden, hidden_few, y_few)


def prepare(ids, weights, out_grad, sections):
    count, part_width = out_grad.shape
    codes = sections * CAP

    def kernel(ids_ref, weights_ref, grad_ref, sent_ref, select_ref, weight_ref):
        live = as_float(ids_ref[...] == 0)
        weight = jnp.sum(live * weights_ref[...], axis=0, keepdims=True)
        live = jnp.sum(live, axis=0, keepdims=True)
        row = iota((count, count), 0)
        col = iota((count, count), 1)
        slot = matmul(jnp.broadcast_to(live, (8, count)), as_float(row < col))[:1]
        slot = jnp.where(live > 0, slot, -1.0)
        at_slot = as_float(slot == row.astype(F32))
        index = iota((8, count), 1).astype(F32) + 1.0
        token = project(index, at_slot) - 1.0
        tile = jnp.concatenate([token, jnp.zeros((8, part_width - count), F32)], 1).astype(BF16)
        sent_ref[:count, :] = grad_ref[...]
        sent_ref[count:, :] = tile
        select_ref[...] = at_slot[:8].astype(BF16)
        parts = jnp.zeros((8, LANES), F32)
        remainder = weight
        for part in range(PARTS):
            piece = remainder.astype(BF16).astype(F32)
            remainder = remainder - piece
            moved = as_float((slot + (codes + part * CAP) == row.astype(F32)) & (slot >= 0))
            parts = parts + project(jnp.broadcast_to(piece, (8, count)), moved)
        weight_ref[...] = parts

    shapes = [((count + 8, part_width), BF16), ((8, count), BF16), ((8, LANES), F32)]
    return pl.pallas_call(
        kernel,
        compiler_params=grant(8),
        in_specs=[whole_spec(value.shape) for value in (ids, weights, out_grad)],
        out_specs=[whole_spec(shape) for shape, _ in shapes],
        out_shape=[jax.ShapeDtypeStruct(shape, dtype) for shape, dtype in shapes],
    )(ids, weights, out_grad)


def halves_of(select):
    low = select.astype(F32)
    return low, pltpu.roll(low, CAP, 0)


def pack_inputs(select, tokens, chips):
    side = tokens.shape[1] // 2

    def kernel(select_ref, tokens_ref, packed_ref):
        low, high = halves_of(select_ref[...])
        rows = (
            matmul(low.astype(BF16), tokens_ref[:, :side])
            + matmul(high.astype(BF16), tokens_ref[:, side:])
        ).astype(BF16)
        for chip in range(chips):
            packed_ref[chip] = rows

    shape = (chips, ROWS, side)
    return pl.pallas_call(
        kernel,
        compiler_params=grant(8),
        in_specs=[whole_spec(select.shape), whole_spec(tokens.shape)],
        out_specs=whole_spec(shape),
        out_shape=jax.ShapeDtypeStruct(shape, BF16),
    )(select, tokens)


def shifts_of(sections):
    return [0] + [way * d for d in range(1, sections // 2) for way in (1, -1)] + [sections // 2]


def pack(where, parts, select, weight, chips):
    sections = len(parts)
    tall, part_width = parts[0].shape
    count = tall - 8
    side = sections * part_width // 2
    codes = sections * CAP
    shifts = shifts_of(sections)

    def kernel(where_ref, *refs):
        part_refs = refs[:sections]
        select_ref, weight_ref, packed_ref, token_ref, rows_ref, tokens_ref = refs[sections:]
        section = where_ref[0]
        low, high = halves_of(select_ref[...])
        rows_ref[...] = jnp.zeros((ROWS, side), F32)
        for shift, ref in zip(shifts, part_refs):
            source = (section + sections - shift) % sections
            chosen = jnp.where(source < sections // 2, low, high).astype(BF16)
            start = source % (sections // 2) * part_width
            spot = pl.ds(pl.multiple_of(start, part_width), part_width)
            rows_ref[:, spot] += matmul(chosen, ref[:count, :])
            tokens_ref[pl.ds(source, 1), :] = ref[count:, :LANES].astype(F32)[:1]
        tokens = tokens_ref[...]
        row = iota((LANES, LANES), 0)
        col = iota((LANES, LANES), 1)
        spread = matmul(tokens, as_float((row < CAP) & (col % CAP == row)))
        lane = iota((sections, LANES), 1)
        layer = iota((sections, LANES), 0)
        pick_lane = lambda size: jnp.sum(
            jnp.where(lane // size == layer, spread, 0.0), axis=0, keepdims=True
        )
        flat = pick_lane(CAP)
        one_lane = lane[:1]
        flat = jnp.where(one_lane < codes, flat, -1.0)
        times = jnp.zeros((1, LANES), F32)
        for slot in range(CAP):
            times = times + jnp.sum(
                as_float(tokens[:, slot : slot + 1] == flat), axis=0, keepdims=True
            )
        times = jnp.where(flat >= 0, times, 0.0)
        code = jnp.where(times > 1, flat, -1.0)
        note = jnp.where(one_lane < codes, code, weight_ref[:1])
        note = jnp.where(one_lane == codes + PARTS * CAP, jnp.max(times), note)
        note = jnp.broadcast_to(note, (ROWS, LANES)).astype(BF16)
        token_ref[...] = jnp.broadcast_to(pick_lane(2 * CAP), (8, LANES))
        rows = rows_ref[...].astype(BF16)
        for chip in range(chips):
            packed_ref[chip, :, :side] = rows
            packed_ref[chip, :, side:] = note

    shapes = [((chips, ROWS, side + LANES), BF16), ((8, LANES), F32)]
    return pl.pallas_call(
        kernel,
        compiler_params=grant(8),
        in_specs=[pl.BlockSpec(memory_space=pltpu.SMEM)]
        + [whole_spec(value.shape) for value in (*parts, select, weight)],
        out_specs=[whole_spec(shape) for shape, _ in shapes],
        out_shape=[jax.ShapeDtypeStruct(shape, dtype) for shape, dtype in shapes],
        scratch_shapes=[pltpu.VMEM((ROWS, side), F32), pltpu.VMEM((sections, LANES), F32)],
    )(where, *parts, select, weight)


def assemble(where, tokens, parts, back):
    sections = len(parts)
    tall, part_width = parts[0].shape
    count = tall - 8
    rows, side = back.shape
    shifts = shifts_of(sections)

    def kernel(where_ref, token_ref, *refs):
        part_refs = refs[:sections]
        back_ref, out_ref = refs[sections:]
        section = where_ref[0]
        lane = iota((count, rows), 1)
        taken = as_float(
            (token_ref[:1, :rows] == iota((count, rows), 0).astype(F32))
            & (lane // (2 * CAP) >= section)
        )
        second = as_float(lane // CAP % 2 == 1)
        for shift, ref in zip(shifts, part_refs):
            source = (section + sections - shift) % sections
            here = jnp.where(source < sections // 2, 1.0 - second, second) * taken
            near = pl.multiple_of(source % (sections // 2) * part_width, part_width)
            added = matmul(here.astype(BF16), back_ref[:, pl.ds(near, part_width)])
            far = pl.multiple_of(source * part_width, part_width)
            out_ref[:, pl.ds(far, part_width)] = (
                ref[:count, :].astype(F32) + added
            ).astype(BF16)

    shape = (count, 2 * side)
    return pl.pallas_call(
        kernel,
        compiler_params=grant(8),
        in_specs=[pl.BlockSpec(memory_space=pltpu.SMEM)]
        + [whole_spec(value.shape) for value in (tokens, *parts, back)],
        out_specs=whole_spec(shape),
        out_shape=jax.ShapeDtypeStruct(shape, BF16),
    )(where, tokens, *parts, back)


def on_device(saved_inputs, expert_ids, gate_weights, out_grad, gate_w, up_w, down_w):
    sections = lax.axis_size("section")
    devices = lax.axis_size("ep")
    chips = devices // 2
    section = lax.axis_index("section")
    place = lax.axis_index("ep")
    core = place % 2
    groups = [[2 * chip + k for chip in range(chips)] for k in range(2)]
    width = saved_inputs.shape[2]
    columns = width // devices
    slots = devices * CAP
    tokens = saved_inputs[0]
    token_count = tokens.shape[0]
    w_gate = gate_w[0]
    w_up = up_w[0]
    w_down = down_w[0]

    where = jnp.stack([section, core, place]).astype(jnp.int32)
    sent, select, slot_weight = prepare(
        expert_ids[0].T, gate_weights[0].T, out_grad, sections
    )

    def around(value, shift):
        pairs = [(i, (i + shift) % sections) for i in range(sections)]
        return lax.ppermute(value, "section", pairs)

    parts = [sent]
    above = below = sent
    for shift in range(1, sections // 2 + 1):
        below = around(below, 1)
        parts.append(below)
        if shift < sections // 2:
            above = around(above, -1)
            parts.append(above)
    x_mine = exchange(pack_inputs(select, tokens, chips), "ep", groups)
    x_mine, parts, select, slot_weight, where = lax.optimization_barrier(
        (x_mine, parts, select, slot_weight, where)
    )
    x_other = from_partner(x_mine, devices)
    packed, all_tokens = pack(where, parts, select, slot_weight, chips)
    y_mine = exchange(packed, "ep", groups)
    y_other = from_partner(y_mine, devices)
    flat = lambda value: value.reshape(chips * ROWS, value.shape[2])

    (
        feeds_few,
        pick_few,
        weight_few,
        notes,
        column,
        x_rows,
        y_rows,
        act,
        slope,
        hidden,
        gate_first,
        up_first,
        act_few,
        slope_few,
        hidden_few,
        gate_few,
        up_few,
        rows_few,
        y_few,
        share_few,
        fits,
        trips,
    ) = first_pass(
        where,
        flat(x_mine),
        flat(x_other),
        flat(y_mine),
        flat(y_other),
        w_gate,
        w_up,
        w_down,
        sections,
    )
    trips = trips.reshape(())

    def slow_plan(size):
        layer_index = jnp.arange(sections, dtype=jnp.int32)
        index = jnp.arange(size, dtype=jnp.int32)
        in_chain = (notes[:, : sections * CAP] >= 0).reshape(devices, sections, CAP)
        flags = jnp.swapaxes(in_chain, 0, 1).reshape(sections, slots)
        within = notes[:, : sections * CAP].astype(jnp.int32).reshape(devices, sections, CAP)
        base = token_count * jnp.arange(devices, dtype=jnp.int32)[:, None, None]
        token = jnp.swapaxes(within + base + 1, 0, 1).reshape(sections, slots)
        place = jnp.cumsum(flags.astype(jnp.int32), axis=1) - 1
        listed = flags[:, None, :] & (place[:, None, :] == index[None, :, None])
        tokens_of = jnp.sum(jnp.where(listed, token[:, None, :], 0), axis=2)
        own_token = lax.dynamic_index_in_dim(tokens_of, section, 0, keepdims=False)
        own = lax.dynamic_index_in_dim(listed, section, 0, keepdims=False)
        parts = notes[:, sections * CAP : (sections + PARTS) * CAP].reshape(devices, PARTS, CAP)
        weight = jnp.sum(jnp.where(own, jnp.sum(parts, axis=1).reshape(1, slots), 0.0), axis=1)
        feeds = (
            (own_token[:, None, None] == tokens_of[None])
            & (own_token[:, None, None] > 0)
            & (layer_index[None, :, None] > section)
        )
        halves = own.reshape(size, 2, chips, CAP)
        halves = jnp.where(core == 0, halves, halves[:, ::-1])
        halves = jnp.concatenate([halves, jnp.zeros_like(halves)], 3)
        return (
            feeds.reshape(size, sections * size).astype(BF16),
            halves.reshape(size, devices * ROWS).astype(BF16),
            jnp.broadcast_to(weight[:, None], (size, LANES)),
        )

    def slow_start(size):
        feeds, pick, weight = slow_plan(size)
        exact = lambda value: lax.dot_general(
            value,
            pick.astype(F32),
            (((1,), (1,)), ((), ())),
            precision=lax.Precision.HIGHEST,
        )
        gate = project(gate_first, pick).astype(BF16)
        up = project(up_first, pick).astype(BF16)
        share = (sum_rows(gate, w_gate) + sum_rows(up, w_up)).astype(BF16)
        return (
            feeds,
            pick,
            weight,
            exact(act),
            exact(slope),
            project(hidden, pick).astype(BF16),
            gate,
            up,
            matmul(pick, column),
            jnp.zeros((size, width), BF16),
            jnp.swapaxes(share.reshape(size, devices, columns), 0, 1),
        )

    def finish(size):
        if size == FEW:
            start = (
                feeds_few,
                pick_few,
                weight_few,
                act_few,
                slope_few,
                hidden_few,
                gate_few,
                up_few,
                rows_few,
                y_few,
                share_few,
            )
        else:
            start = slow_start(size)
        feeds, pick, weight, act_rows, slope_rows, hidden_rows = start[:6]
        first_rows = start[8]

        def more(state):
            return state[0] < trips

        def step(state):
            trip = state[0] + 1
            last = (trip >= trips).astype(jnp.int32).reshape(1)
            share, trip, last = lax.optimization_barrier((state[4], trip, last))
            summed = jnp.sum(exchange(share, "ep").astype(F32), axis=0)
            high = lax.reduce_precision(summed, 8, 7)
            summed = jnp.concatenate([high.astype(BF16), (summed - high).astype(BF16)], 0)
            layers = exchange(repeated(summed, sections), "section")
            blocks = exchange(chain_rows(layers, feeds, first_rows, weight, devices), "ep")
            y, gate, up, share = chain_step(last, blocks, act_rows, slope_rows, w_gate, w_up, w_down)
            return (trip, y, gate, up, share)

        state = (jnp.int32(0), start[9], start[6], start[7], start[10])
        _, y, gate, up, _ = lax.while_loop(more, step, state)
        gate, up, hidden_kept, share_mine, share_other = merge_chains(
            pick, gate_first, up_first, hidden, gate, up, w_gate, w_up
        )

        theirs = from_partner(share_other, devices)
        chip_sum = (share_mine.astype(F32) + theirs.astype(F32)).astype(BF16)
        tiles = exchange(chip_sum.reshape(chips, ROWS, width // 2), "ep", groups)
        back = lax.reduce_precision(jnp.sum(tiles.astype(F32), axis=0), 8, 7).astype(BF16)
        grads = weight_gradients(
            x_rows, y_rows, gate, up, hidden_kept, hidden_rows, y
        )
        spread, grads = lax.optimization_barrier((repeated(back, sections), grads))
        all_back = exchange(spread, "section")
        result = assemble(where, all_tokens, parts, all_back.reshape(sections * ROWS, width // 2))
        return (result, *grads)

    outputs = lax.cond(fits.reshape(()) != 0, lambda: finish(FEW), lambda: finish(slots))
    return tuple(output[None] for output in outputs)


def solution(mesh):
    by_rows = P("section", "ep", None)
    return jax.shard_map(
        on_device,
        mesh=mesh,
        in_specs=(by_rows, by_rows, by_rows, P("ep", "section"), by_rows, by_rows, by_rows),
        out_specs=(by_rows, by_rows, by_rows, by_rows),
        check_vma=False,
    )
```

profile of v0, /device:TPU:1, one launch (start us, length us, event | category | flops | bytes accessed | tf_op | source)
XLA Modules:
  0.0 184.9 jit_solution(3483955943300453317)
XLA Ops:
  3.2 2.5 %collective-permute-start.2 = (bf16[136,512]{1,0:T(8,128)(2,1)S(1)}, bf16[136,512]{1,0:T(8,128)(2,1)S(1)}, u32[]{:S(2)}, u32[]{:S(2)}) collective-permute-start(bf16[136,512]{1,0:T(8,128)(2,1)S(1)} %get-tuple-element.400.refs_0_), channel_id=1, source_target_pairs={{0,32},{32,64},{64,96},{96,128},{128,160},{160,192},{192,224},{224... | collective-permute-start | bytes 417800 | tf_op jit(solution)/shard_map/ppermute | solution.py:592
  5.7 1.2 copy-done
  6.9 1.1 shard_map.103
  8.0 6.9 %all-to-all-start.10 = ((bf16[16,8,2048]{2,1,0:T(8,128)(2,1)}), bf16[16,8,2048]{2,1,0:T(8,128)(2,1)S(1)}, u32[]{:S(2)}, u32[]{:S(2)}) async-start(bf16[16,8,2048]{2,1,0:T(8,128)(2,1)} %shard_map.103), calls=%async_computation.10 | async-start | bytes 1048576 | tf_op jit(solution)/shard_map/all_to_all | solution.py:19
  14.8 4.0 %collective-permute-start.3 = (bf16[136,512]{1,0:T(8,128)(2,1)S(1)}, bf16[136,512]{1,0:T(8,128)(2,1)S(1)}, u32[]{:S(2)}, u32[]{:S(2)}) collective-permute-start(bf16[136,512]{1,0:T(8,128)(2,1)S(1)} %get-tuple-element.400.refs_0_), channel_id=1, source_target_pairs={{0,224},{32,0},{64,32},{96,64},{128,96},{160,128},{192,160},{224,1... | collective-permute-start | bytes 417800 | tf_op jit(solution)/shard_map/ppermute | solution.py:592
  18.9 2.0 %collective-permute-done.3.refs_2_ = bf16[136,512]{1,0:T(8,128)(2,1)S(1)} collective-permute-done((bf16[136,512]{1,0:T(8,128)(2,1)S(1)}, bf16[136,512]{1,0:T(8,128)(2,1)S(1)}, u32[]{:S(2)}, u32[]{:S(2)}) %collective-permute-start.3) | collective-permute-done | bytes 139296 | tf_op jit(solution)/shard_map/ppermute | solution.py:592
  20.9 3.5 %collective-permute-start.5 = (bf16[136,512]{1,0:T(8,128)(2,1)S(1)}, bf16[136,512]{1,0:T(8,128)(2,1)S(1)}, u32[]{:S(2)}, u32[]{:S(2)}) collective-permute-start(bf16[136,512]{1,0:T(8,128)(2,1)S(1)} %collective-permute-done.3.refs_2_), channel_id=1, source_target_pairs={{0,224},{32,0},{64,32},{96,64},{128,96},{160,128},{192,160},{224,1... | collective-permute-start | bytes 417800 | tf_op jit(solution)/shard_map/ppermute | solution.py:592
  24.4 2.0 %collective-permute-done.5.refs_4_ = bf16[136,512]{1,0:T(8,128)(2,1)S(1)} collective-permute-done((bf16[136,512]{1,0:T(8,128)(2,1)S(1)}, bf16[136,512]{1,0:T(8,128)(2,1)S(1)}, u32[]{:S(2)}, u32[]{:S(2)}) %collective-permute-start.5) | collective-permute-done | bytes 139296 | tf_op jit(solution)/shard_map/ppermute | solution.py:592
  26.4 3.4 %collective-permute-start.7 = (bf16[136,512]{1,0:T(8,128)(2,1)S(1)}, bf16[136,512]{1,0:T(8,128)(2,1)S(1)}, u32[]{:S(2)}, u32[]{:S(2)}) collective-permute-start(bf16[136,512]{1,0:T(8,128)(2,1)S(1)} %collective-permute-done.5.refs_4_), channel_id=1, source_target_pairs={{0,224},{32,0},{64,32},{96,64},{128,96},{160,128},{192,160},{224,1... | collective-permute-start | bytes 417800 | tf_op jit(solution)/shard_map/ppermute | solution.py:592
  29.9 1.9 %collective-permute-done.7.refs_6_ = bf16[136,512]{1,0:T(8,128)(2,1)S(1)} collective-permute-done((bf16[136,512]{1,0:T(8,128)(2,1)S(1)}, bf16[136,512]{1,0:T(8,128)(2,1)S(1)}, u32[]{:S(2)}, u32[]{:S(2)}) %collective-permute-start.7) | collective-permute-done | bytes 139296 | tf_op jit(solution)/shard_map/ppermute | solution.py:592
  31.8 3.1 %collective-permute-done.8.refs_7_ = bf16[136,512]{1,0:T(8,128)(2,1)S(1)} collective-permute-done((bf16[136,512]{1,0:T(8,128)(2,1)S(1)}, bf16[136,512]{1,0:T(8,128)(2,1)S(1)}, u32[]{:S(2)}, u32[]{:S(2)}) %collective-permute-start.8) | collective-permute-done | bytes 139296 | tf_op jit(solution)/shard_map/ppermute | solution.py:592
  34.9 1.4 shard_map.104
  36.3 15.3 %all_to_all.67 = bf16[16,8,2176]{2,1,0:T(8,128)(2,1)S(1)} all-to-all(bf16[16,8,2176]{2,1,0:T(8,128)(2,1)S(1)} %get-tuple-element.410), channel_id=1, replica_groups={{0,2,4,6,8,10,12,14,16,18,20,22,24,26,28,30},{1,3,5,7,9,11,13,15,17,19,..., dimensions={0} | all-to-all | bytes 1114112 | tf_op jit(solution)/shard_map/all_to_all | solution.py:19
  51.6 6.1 %collective-permute-start.10 = (bf16[16,8,2176]{2,1,0:T(8,128)(2,1)S(1)}, bf16[16,8,2176]{2,1,0:T(8,128)(2,1)S(1)}, u32[]{:S(2)}, u32[]{:S(2)}) collective-permute-start(bf16[16,8,2176]{2,1,0:T(8,128)(2,1)S(1)} %all_to_all.67), channel_id=1, source_target_pairs={{0,1},{1,0},{2,3},{3,2},{4,5},{5,4},{6,7},{7,6},{8,9},{9,8},{10,11... | collective-permute-start | bytes 1671176 | tf_op jit(solution)/shard_map/ppermute | solution.py:27
  57.7 2.3 %collective-permute-done.9 = bf16[16,8,2048]{2,1,0:T(8,128)(2,1)S(1)} collective-permute-done((bf16[16,8,2048]{2,1,0:T(8,128)(2,1)S(1)}, bf16[16,8,2048]{2,1,0:T(8,128)(2,1)S(1)}, u32[]{:S(2)}, u32[]{:S(2)}) %collective-permute-start.9) | collective-permute-done | bytes 524320 | tf_op jit(solution)/shard_map/ppermute | solution.py:27
  60.1 6.8 %shard_map.105 = (bf16[16,128]{1,0:T(8,128)(2,1)}, bf16[16,256]{1,0:T(8,128)(2,1)}, f32[16,128]{1,0:T(8,128)S(1)}, f32[32,128]{1,0:T(8,128)S(1)}, bf16[256,128]{...) custom-call(s32[3]{0:T(128)} %copy-done.49, ...), custom_call_target="tpu_custom_call" | custom-call | tf_op jit(solution)/shard_map/pallas_call | solution.py:244
  67.5 116.5 %conditional.1 = (bf16[224,4096]{1,0:T(8,128)(2,1)}, bf16[224,4096]{1,0:T(8,128)(2,1)}, bf16[224,4096]{1,0:T(8,128)(2,1)}, bf16[1,128,4096]{2,1,0:T(8,128)(2,1)S(1)}) conditional(s32[]{:T(128)} %bitcast.40, (s32[]{:T(128)}, f32[32,128]{1,0:T(8,128)S(1)}, s32[]{:T(128)}, bf16[224,256]{1,0:T(8,128)(2,1)}, bf16[224,256]{1,0:T(8,128)(2,1)}, ...), branch_computations={%region_0.9_spmd, %region_9.14_spmd} | conditional | flops 703832320 | bytes 64377592 | solution.py:755
  68.6 82.2 %while.31 = (s32[]{:T(128)}, bf16[16,4096]{1,0:T(8,128)(2,1)}, bf16[224,16]{1,0:T(8,128)(2,1)}, bf16[224,16]{1,0:T(8,128)(2,1)}, bf16[32,16,128]{2,1,0:T(8,128)(...) while((s32[]{:T(128)}, bf16[16,4096]{1,0:T(8,128)(2,1)}, ...), condition=%wide.region_12.12_spmd, body=%wide.region_10.11_spmd.sunk | while | flops 153604 | bytes 901275 | solution.py:738
  69.9 11.2 %all_to_all.68 = bf16[32,16,128]{2,1,0:T(8,128)(2,1)S(1)} all-to-all(bf16[32,16,128]{2,1,0:T(8,128)(2,1)S(1)} %get-tuple-element.789), channel_id=1, replica_groups=mesh['section'=8,'ep'=32] {'ep'}, dimensions={0} | all-to-all | bytes 262144 | tf_op jit(solution)/shard_map/cond/branch_1_fun/while/body/all_to_all | solution.py:19
  81.2 12.6 %all_to_all.69.layers_ref = bf16[8,32,128]{2,1,0:T(8,128)(2,1)S(1)} all-to-all(bf16[8,32,128]{2,1,0:T(8,128)(2,1)S(1)} %broadcast_in_dim.96), channel_id=1, replica_groups=mesh['section'=8,'ep'=32] {'section'}, dimensions={0} | all-to-all | bytes 131072 | tf_op jit(solution)/shard_map/cond/branch_1_fun/while/body/all_to_all | solution.py:19
  94.7 12.7 %all_to_all.70.blocks_ref = bf16[32,16,128]{2,1,0:T(8,128)(2,1)S(1)} all-to-all(bf16[32,16,128]{2,1,0:T(8,128)(2,1)S(1)} %body.4), channel_id=1, replica_groups=mesh['section'=8,'ep'=32] {'ep'}, dimensions={0} | all-to-all | bytes 262144 | tf_op jit(solution)/shard_map/cond/branch_1_fun/while/body/all_to_all | solution.py:19
  107.3 4.0 %body.5 = (bf16[16,4096]{1,0:T(8,128)(2,1)}, bf16[224,16]{1,0:T(8,128)(2,1)}, bf16[224,16]{1,0:T(8,128)(2,1)}, bf16[32,16,128]{2,1,0:T(8,128)(2,1)S(1)}) custom-call(s32[1]{0:T(128)} %bitcast.86.last_ref, bf16[32,16,128]{2,1,0:T(8,128)(2,1)S(1)} %all_to_all.70.blocks_ref, f32[224,16]{1,0:T(8,128)S(1)} %get-tuple-element.858.act_ref, ...), custom_call_target="tpu_custom_call" | custom-call | tf_op jit(solution)/shard_map/cond/branch_1_fun/while/body/pallas_call | solution.py:314
  112.6 11.2 %all_to_all.68 = bf16[32,16,128]{2,1,0:T(8,128)(2,1)S(1)} all-to-all(bf16[32,16,128]{2,1,0:T(8,128)(2,1)S(1)} %get-tuple-element.789), channel_id=1, replica_groups=mesh['section'=8,'ep'=32] {'ep'}, dimensions={0} | all-to-all | bytes 262144 | tf_op jit(solution)/shard_map/cond/branch_1_fun/while/body/all_to_all | solution.py:19
  123.9 9.5 %all_to_all.69.layers_ref = bf16[8,32,128]{2,1,0:T(8,128)(2,1)S(1)} all-to-all(bf16[8,32,128]{2,1,0:T(8,128)(2,1)S(1)} %broadcast_in_dim.96), channel_id=1, replica_groups=mesh['section'=8,'ep'=32] {'section'}, dimensions={0} | all-to-all | bytes 131072 | tf_op jit(solution)/shard_map/cond/branch_1_fun/while/body/all_to_all | solution.py:19
  134.4 12.5 %all_to_all.70.blocks_ref = bf16[32,16,128]{2,1,0:T(8,128)(2,1)S(1)} all-to-all(bf16[32,16,128]{2,1,0:T(8,128)(2,1)S(1)} %body.4), channel_id=1, replica_groups=mesh['section'=8,'ep'=32] {'ep'}, dimensions={0} | all-to-all | bytes 262144 | tf_op jit(solution)/shard_map/cond/branch_1_fun/while/body/all_to_all | solution.py:19
  146.9 3.4 %body.5 = (bf16[16,4096]{1,0:T(8,128)(2,1)}, bf16[224,16]{1,0:T(8,128)(2,1)}, bf16[224,16]{1,0:T(8,128)(2,1)}, bf16[32,16,128]{2,1,0:T(8,128)(2,1)S(1)}) custom-call(s32[1]{0:T(128)} %bitcast.86.last_ref, bf16[32,16,128]{2,1,0:T(8,128)(2,1)S(1)} %all_to_all.70.blocks_ref, f32[224,16]{1,0:T(8,128)S(1)} %get-tuple-element.858.act_ref, ...), custom_call_target="tpu_custom_call" | custom-call | tf_op jit(solution)/shard_map/cond/branch_1_fun/while/body/pallas_call | solution.py:314
  150.9 3.2 %branch_1_fun.3 = (bf16[2,224,256]{2,1,0:T(8,128)(2,1)S(1)}, bf16[2,224,256]{2,1,0:T(8,128)(2,1)S(1)}, bf16[2,224,256]{2,1,0:T(8,128)(2,1)S(1)}, bf16[128,2048]{1,0:T(8,128)(2,1)S(1)}, bf16[128,2048]{1,0:T(8,128)(2,1)S(1)}) custom-call(bf16[16,256]{1,0:T(8,128)(2,1)} %get-tuple-element.303.pick_ref, bf16[224,256]{1,0:T(8,128)(2,1)} %get-tuple-element.304.gate_ref, ...), custom_call_target="tpu_custom_call" | custom-call | tf_op jit(solution)/shard_map/cond/branch_1_fun/pallas_call | solution.py:364
  154.6 1.5 collective-permute-done
  157.1 3.6 %all-to-all-start.3 = ((bf16[16,8,2048]{2,1,0:T(8,128)(2,1)}), bf16[16,8,2048]{2,1,0:T(8,128)(2,1)S(1)}, u32[]{:S(2)}, u32[]{:S(2)}) async-start(bf16[16,8,2048]{2,1,0:T(8,128)(2,1)} %fusion.5), calls=%async_computation.3 | async-start | bytes 1048576 | tf_op jit(solution)/shard_map/cond/branch_1_fun/all_to_all | solution.py:19
  160.8 7.4 %branch_1_fun.4 = (bf16[224,4096]{1,0:T(8,128)(2,1)}, bf16[224,4096]{1,0:T(8,128)(2,1)}, bf16[224,4096]{1,0:T(8,128)(2,1)}) custom-call(bf16[256,2048]{1,0:T(8,128)(2,1)S(1)} %copy-done.9, bf16[256,2048]{1,0:T(8,128)(2,1)} %get-tuple-element.325.y_ref, bf16[2,224,256]{2,1,0:T(8,128)(2,1)S(1)} %get-tuple-element.326.gate_ref, ...), custom_call_target="tpu_custom_call" | custom-call | tf_op jit(solution)/shard_map/cond/branch_1_fun/pallas_call | solution.py:389
  168.1 2.7 %all-to-all-done.3 = bf16[16,8,2048]{2,1,0:T(8,128)(2,1)S(1)} async-done(((bf16[16,8,2048]{2,1,0:T(8,128)(2,1)}), bf16[16,8,2048]{2,1,0:T(8,128)(2,1)S(1)}, u32[]{:S(2)}, u32[]{:S(2)}) %all-to-all-start.3) | async-done | bytes 524320 | tf_op jit(solution)/shard_map/cond/branch_1_fun/all_to_all | solution.py:19
  171.0 12.0 %all_to_all.66 = bf16[8,8,2048]{2,1,0:T(8,128)(2,1)S(1)} all-to-all(bf16[8,8,2048]{2,1,0:T(8,128)(2,1)S(1)} %broadcast_in_dim.72), channel_id=1, replica_groups=mesh['section'=8,'ep'=32] {'section'}, dimensions={0} | all-to-all | bytes 524288 | tf_op jit(solution)/shard_map/cond/branch_1_fun/all_to_all | solution.py:19
  (82 shorter events, 8.9 us)
Async XLA Ops:
  3.2 15.7 %collective-permute-start.2 = (bf16[136,512]{1,0:T(8,128)(2,1)S(1)}, bf16[136,512]{1,0:T(8,128)(2,1)S(1)}, u32[]{:S(2)}, u32[]{:S(2)}) collective-permute-start(bf16[136,512]{1,0:T(8,128)(2,1)S(1)} %get-tuple-element.400.refs_0_), channel_id=1, source_target_pairs={{0,32},{32,64},{64,96},{96,128},{128,160},{160,192},{192,224},{224... | collective-permute-start | bytes 417800 | tf_op jit(solution)/shard_map/ppermute | solution.py:592
  5.7 1.2 copy-start
  8.0 52.1 %copy-start.4 = (bf16[1,224,4096]{2,1,0:T(8,128)(2,1)S(1)}, bf16[1,224,4096]{2,1,0:T(8,128)(2,1)}, u32[]{:S(2)}) copy-start(bf16[1,224,4096]{2,1,0:T(8,128)(2,1)} %param.17) | copy-start | bytes 5505028
  8.0 23.8 %all-to-all-start.10 = ((bf16[16,8,2048]{2,1,0:T(8,128)(2,1)}), bf16[16,8,2048]{2,1,0:T(8,128)(2,1)S(1)}, u32[]{:S(2)}, u32[]{:S(2)}) async-start(bf16[16,8,2048]{2,1,0:T(8,128)(2,1)} %shard_map.103), calls=%async_computation.10 | async-start | bytes 1048576 | tf_op jit(solution)/shard_map/all_to_all | solution.py:19
  14.8 6.0 %collective-permute-start.3 = (bf16[136,512]{1,0:T(8,128)(2,1)S(1)}, bf16[136,512]{1,0:T(8,128)(2,1)S(1)}, u32[]{:S(2)}, u32[]{:S(2)}) collective-permute-start(bf16[136,512]{1,0:T(8,128)(2,1)S(1)} %get-tuple-element.400.refs_0_), channel_id=1, source_target_pairs={{0,224},{32,0},{64,32},{96,64},{128,96},{160,128},{192,160},{224,1... | collective-permute-start | bytes 417800 | tf_op jit(solution)/shard_map/ppermute | solution.py:592
  18.9 5.5 %collective-permute-start.4 = (bf16[136,512]{1,0:T(8,128)(2,1)S(1)}, bf16[136,512]{1,0:T(8,128)(2,1)S(1)}, u32[]{:S(2)}, u32[]{:S(2)}) collective-permute-start(bf16[136,512]{1,0:T(8,128)(2,1)S(1)} %collective-permute-done.2.refs_1_), channel_id=1, source_target_pairs={{0,32},{32,64},{64,96},{96,128},{128,160},{160,192},{192,224},{224... | collective-permute-start | bytes 417800 | tf_op jit(solution)/shard_map/ppermute | solution.py:592
  20.9 5.5 %collective-permute-start.5 = (bf16[136,512]{1,0:T(8,128)(2,1)S(1)}, bf16[136,512]{1,0:T(8,128)(2,1)S(1)}, u32[]{:S(2)}, u32[]{:S(2)}) collective-permute-start(bf16[136,512]{1,0:T(8,128)(2,1)S(1)} %collective-permute-done.3.refs_2_), channel_id=1, source_target_pairs={{0,224},{32,0},{64,32},{96,64},{128,96},{160,128},{192,160},{224,1... | collective-permute-start | bytes 417800 | tf_op jit(solution)/shard_map/ppermute | solution.py:592
  24.4 5.4 %collective-permute-start.6 = (bf16[136,512]{1,0:T(8,128)(2,1)S(1)}, bf16[136,512]{1,0:T(8,128)(2,1)S(1)}, u32[]{:S(2)}, u32[]{:S(2)}) collective-permute-start(bf16[136,512]{1,0:T(8,128)(2,1)S(1)} %collective-permute-done.4.refs_3_), channel_id=1, source_target_pairs={{0,32},{32,64},{64,96},{96,128},{128,160},{160,192},{192,224},{224... | collective-permute-start | bytes 417800 | tf_op jit(solution)/shard_map/ppermute | solution.py:592
  26.4 5.4 %collective-permute-start.7 = (bf16[136,512]{1,0:T(8,128)(2,1)S(1)}, bf16[136,512]{1,0:T(8,128)(2,1)S(1)}, u32[]{:S(2)}, u32[]{:S(2)}) collective-permute-start(bf16[136,512]{1,0:T(8,128)(2,1)S(1)} %collective-permute-done.5.refs_4_), channel_id=1, source_target_pairs={{0,224},{32,0},{64,32},{96,64},{128,96},{160,128},{192,160},{224,1... | collective-permute-start | bytes 417800 | tf_op jit(solution)/shard_map/ppermute | solution.py:592
  29.8 30.3 %copy-start.30 = (bf16[136,512]{1,0:T(8,128)(2,1)}, bf16[136,512]{1,0:T(8,128)(2,1)S(1)}, u32[]{:S(2)}) copy-start(bf16[136,512]{1,0:T(8,128)(2,1)S(1)} %collective-permute-done.6.refs_5_) | copy-start | bytes 417796
  29.8 5.1 %collective-permute-start.8 = (bf16[136,512]{1,0:T(8,128)(2,1)S(1)}, bf16[136,512]{1,0:T(8,128)(2,1)S(1)}, u32[]{:S(2)}, u32[]{:S(2)}) collective-permute-start(bf16[136,512]{1,0:T(8,128)(2,1)S(1)} %collective-permute-done.6.refs_5_), channel_id=1, source_target_pairs={{0,32},{32,64},{64,96},{96,128},{128,160},{160,192},{192,224},{224... | collective-permute-start | bytes 417800 | tf_op jit(solution)/shard_map/ppermute | solution.py:592
  29.9 30.2 %copy-start.49 = (s32[3]{0:T(128)}, s32[3]{0:T(128)S(1)}, u32[]{:S(2)}) copy-start(s32[3]{0:T(128)S(1)} %pad_add_fusion.where_ref) | copy-start | bytes 40
  31.8 28.2 %copy-start.33 = (bf16[136,512]{1,0:T(8,128)(2,1)}, bf16[136,512]{1,0:T(8,128)(2,1)S(1)}, u32[]{:S(2)}) copy-start(bf16[136,512]{1,0:T(8,128)(2,1)S(1)} %collective-permute-done.7.refs_6_) | copy-start | bytes 417796
  34.9 25.2 %copy-start.36 = (bf16[136,512]{1,0:T(8,128)(2,1)}, bf16[136,512]{1,0:T(8,128)(2,1)S(1)}, u32[]{:S(2)}) copy-start(bf16[136,512]{1,0:T(8,128)(2,1)S(1)} %collective-permute-done.8.refs_7_) | copy-start | bytes 417796
  51.6 8.4 %collective-permute-start.10 = (bf16[16,8,2176]{2,1,0:T(8,128)(2,1)S(1)}, bf16[16,8,2176]{2,1,0:T(8,128)(2,1)S(1)}, u32[]{:S(2)}, u32[]{:S(2)}) collective-permute-start(bf16[16,8,2176]{2,1,0:T(8,128)(2,1)S(1)} %all_to_all.67), channel_id=1, source_target_pairs={{0,1},{1,0},{2,3},{3,2},{4,5},{5,4},{6,7},{7,6},{8,9},{9,8},{10,11... | collective-permute-start | bytes 1671176 | tf_op jit(solution)/shard_map/ppermute | solution.py:27
  57.7 2.3 %collective-permute-start.9 = (bf16[16,8,2048]{2,1,0:T(8,128)(2,1)S(1)}, bf16[16,8,2048]{2,1,0:T(8,128)(2,1)S(1)}, u32[]{:S(2)}, u32[]{:S(2)}) collective-permute-start(bf16[16,8,2048]{2,1,0:T(8,128)(2,1)S(1)} %all-to-all-done.10), channel_id=1, source_target_pairs={{0,1},{1,0},{2,3},{3,2},{4,5},{5,4},{6,7},{7,6},{8,9},{9,8},{10,11... | collective-permute-start | bytes 1572872 | tf_op jit(solution)/shard_map/ppermute | solution.py:27
  67.8 83.1 %copy-start.41 = (bf16[224,256]{1,0:T(8,128)(2,1)S(1)}, bf16[224,256]{1,0:T(8,128)(2,1)}, u32[]{:S(2)}) copy-start(bf16[224,256]{1,0:T(8,128)(2,1)} %get-tuple-element.306.hidden_ref) | copy-start | bytes 344068 | tf_op jit(solution)/shard_map/cond
  154.1 6.5 %copy-start.9 = (bf16[256,2048]{1,0:T(8,128)(2,1)S(1)}, bf16[256,2048]{1,0:T(8,128)(2,1)}, u32[]{:S(2)}) copy-start(bf16[256,2048]{1,0:T(8,128)(2,1)} %get-tuple-element.324.x_ref) | copy-start | bytes 3145732 | tf_op jit(solution)/shard_map/cond
  154.1 6.5 %copy-start.46 = (bf16[224,16]{1,0:T(8,128)(2,1)S(1)}, bf16[224,16]{1,0:T(8,128)(2,1)}, u32[]{:S(2)}) copy-start(bf16[224,16]{1,0:T(8,128)(2,1)} %get-tuple-element.329.hf_ref) | copy-start | bytes 21508 | tf_op jit(solution)/shard_map/cond
  154.2 2.0 %collective-permute-start = (bf16[128,2048]{1,0:T(8,128)(2,1)S(1)}, bf16[128,2048]{1,0:T(8,128)(2,1)S(1)}, u32[]{:S(2)}, u32[]{:S(2)}) collective-permute-start(bf16[128,2048]{1,0:T(8,128)(2,1)S(1)} %get-tuple-element.323), channel_id=1, source_target_pairs={{0,1},{1,0},{2,3},{3,2},{4,5},{5,4},{6,7},{7,6},{8,9},{9,8},{10,11... | collective-permute-start | bytes 1572872 | tf_op jit(solution)/shard_map/cond/branch_1_fun/ppermute | solution.py:27
  157.1 13.7 %all-to-all-start.3 = ((bf16[16,8,2048]{2,1,0:T(8,128)(2,1)}), bf16[16,8,2048]{2,1,0:T(8,128)(2,1)S(1)}, u32[]{:S(2)}, u32[]{:S(2)}) async-start(bf16[16,8,2048]{2,1,0:T(8,128)(2,1)} %fusion.5), calls=%async_computation.3 | async-start | bytes 1048576 | tf_op jit(solution)/shard_map/cond/branch_1_fun/all_to_all | solution.py:19
  160.7 22.2 %copy-start.13 = (bf16[136,512]{1,0:T(8,128)(2,1)S(1)}, bf16[136,512]{1,0:T(8,128)(2,1)}, u32[]{:S(2)}) copy-start(bf16[136,512]{1,0:T(8,128)(2,1)} %copy-done.12) | copy-start | bytes 417796 | tf_op jit(solution)/shard_map/cond
  160.7 22.2 %copy-start.17 = (bf16[136,512]{1,0:T(8,128)(2,1)S(1)}, bf16[136,512]{1,0:T(8,128)(2,1)}, u32[]{:S(2)}) copy-start(bf16[136,512]{1,0:T(8,128)(2,1)} %copy-done.16) | copy-start | bytes 417796 | tf_op jit(solution)/shard_map/cond
  160.7 22.2 %copy-start.21 = (bf16[136,512]{1,0:T(8,128)(2,1)S(1)}, bf16[136,512]{1,0:T(8,128)(2,1)}, u32[]{:S(2)}) copy-start(bf16[136,512]{1,0:T(8,128)(2,1)} %copy-done.20) | copy-start | bytes 417796 | tf_op jit(solution)/shard_map/cond
  160.7 22.2 %copy-start.25 = (bf16[136,512]{1,0:T(8,128)(2,1)S(1)}, bf16[136,512]{1,0:T(8,128)(2,1)}, u32[]{:S(2)}) copy-start(bf16[136,512]{1,0:T(8,128)(2,1)} %copy-done.24) | copy-start | bytes 417796 | tf_op jit(solution)/shard_map/cond
  160.7 22.2 %copy-start.29 = (bf16[136,512]{1,0:T(8,128)(2,1)S(1)}, bf16[136,512]{1,0:T(8,128)(2,1)}, u32[]{:S(2)}) copy-start(bf16[136,512]{1,0:T(8,128)(2,1)} %copy-done.28) | copy-start | bytes 417796 | tf_op jit(solution)/shard_map/cond
  160.7 22.2 %copy-start.32 = (bf16[136,512]{1,0:T(8,128)(2,1)S(1)}, bf16[136,512]{1,0:T(8,128)(2,1)}, u32[]{:S(2)}) copy-start(bf16[136,512]{1,0:T(8,128)(2,1)} %get-tuple-element.344.refs_5_) | copy-start | bytes 417796 | tf_op jit(solution)/shard_map/cond
  160.8 22.2 %copy-start.35 = (bf16[136,512]{1,0:T(8,128)(2,1)S(1)}, bf16[136,512]{1,0:T(8,128)(2,1)}, u32[]{:S(2)}) copy-start(bf16[136,512]{1,0:T(8,128)(2,1)} %get-tuple-element.345.refs_6_) | copy-start | bytes 417796 | tf_op jit(solution)/shard_map/cond
  160.8 22.2 %copy-start.38 = (bf16[136,512]{1,0:T(8,128)(2,1)S(1)}, bf16[136,512]{1,0:T(8,128)(2,1)}, u32[]{:S(2)}) copy-start(bf16[136,512]{1,0:T(8,128)(2,1)} %get-tuple-element.346.refs_7_) | copy-start | bytes 417796 | tf_op jit(solution)/shard_map/cond
  160.8 22.2 %copy-start.48 = (f32[8,128]{1,0:T(8,128)S(1)}, f32[8,128]{1,0:T(8,128)}, u32[]{:S(2)}) copy-start(f32[8,128]{1,0:T(8,128)} %get-tuple-element.338.token_ref) | copy-start | bytes 12292 | tf_op jit(solution)/shard_map/cond
  160.8 22.2 %copy-start.51 = (s32[3]{0:T(128)S(1)}, s32[3]{0:T(128)}, u32[]{:S(2)}) copy-start(s32[3]{0:T(128)} %get-tuple-element.337.where_ref) | copy-start | bytes 40 | tf_op jit(solution)/shard_map/cond
  184.0 1.0 copy-start.39
  (8 other events, 6.0 us)
where the time goes:
time: 187 us; the launch traced here: 185 us
  blocking collectives  96.9 us (52%)
  starting transfers between devices  30.4 us (16%)
  Pallas kernels  30.3 us (16%)
  waiting for transfers between devices  15.6 us (8%)
  local copies, waits for them, and re-layouts  5.38 us (3%)
  loops' own time  3.74 us (2%)
    all_to_all x8, blocking collectives, exchange(): lax.all_to_all(blocks, axis, 0, 0, tiled=True, axis_index_groups=groups)  96.9 us
    ppermute x7, starting transfers between devices, around(): return lax.ppermute(value, 'section', pairs)  13.3 us
    all_to_all x2, starting transfers between devices, exchange(): lax.all_to_all(blocks, axis, 0, 0, tiled=True, axis_index_groups=groups)  10.5 us
    ppermute x7, waiting for transfers between devices, around(): return lax.ppermute(value, 'section', pairs)  9.06 us
    pallas_call x2, Pallas kernels, chain_step(): pl.pallas_call(kernel, compiler_params=grant(16), in_specs=[pl.BlockSpec(...  7.38 us
    pallas_call x1, Pallas kernels, weight_gradients(): pl.pallas_call(kernel, compiler_params=grant(16), grid=(width // block,),...  7.35 us
    pallas_call x1, Pallas kernels, first_pass(): pl.pallas_call(kernel, compiler_params=grant(28), in_specs=[smem] + [whol...  6.79 us
    ppermute x3, starting transfers between devices, from_partner(): return lax.ppermute(value, 'ep', [(i, i ^ 1) for i in range(devices)])  6.58 us
  transfers between devices with their start and end apart: 12, of which 7 were waited for; matrix products, arithmetic and copies ran while one was open for 0% of the time, Pallas kernels for 5%

commit v1 on v0

--- a/solution.py
+++ b/solution.py
@@ -287,14 +287,27 @@
         blocks_ref,
         act_ref,
         slope_ref,
-        w_gate_ref,
-        w_up_ref,
+        gate_hbm,
+        up_hbm,
         w_down_ref,
         y_ref,
         gate_few_ref,
         up_few_ref,
         share_ref,
+        w_gate_ref,
+        w_up_ref,
+        sems,
     ):
+        copies = [
+            pltpu.make_async_copy(gate_hbm, w_gate_ref, sems.at[0]),
+            pltpu.make_async_copy(up_hbm, w_up_ref, sems.at[1]),
+        ]
+
+        @pl.when(last_ref[0] == 0)
+        def _():
+            for copy in copies:
+                copy.start()
+
         for index in range(devices):
             y_ref[:, index * columns : (index + 1) * columns] = blocks_ref[index]
         grad = project(w_down_ref[...], y_ref[...])
@@ -305,6 +318,8 @@
 
         @pl.when(last_ref[0] == 0)
         def _():
+            for copy in copies:
+                copy.wait()
             share = sum_rows(gate_few, w_gate_ref[...])
             share = (share + sum_rows(up_few, w_up_ref[...])).astype(BF16)
             for index in range(devices):
@@ -316,9 +331,15 @@
         compiler_params=grant(16),
         in_specs=[pl.BlockSpec(memory_space=pltpu.SMEM)]
         + [whole_spec(value.shape) for value in (y_blocks, act_few, slope_few)]
-        + [whole_spec(w_gate.shape)] * 3,
+        + [pl.BlockSpec(memory_space=pl.ANY)] * 2
+        + [whole_spec(w_down.shape)],
         out_specs=[whole_spec(shape) for shape in shapes],
         out_shape=[jax.ShapeDtypeStruct(shape, BF16) for shape in shapes],
+        scratch_shapes=[
+            pltpu.VMEM(w_gate.shape, BF16),
+            pltpu.VMEM(w_up.shape, BF16),
+            pltpu.SemaphoreType.DMA((2,)),
+        ],
     )(last, y_blocks, act_few, slope_few, w_gate, w_up, w_down)
 
 

time: 187 us -> 187 us (level)
  no operation moved by 1% of the time
where the time goes in v1:
time: 187 us; the launch traced here: 185 us
  blocking collectives  96.9 us (52%)
  starting transfers between devices  30.4 us (16%)
  Pallas kernels  30.3 us (16%)
  waiting for transfers between devices  15.6 us (8%)
  local copies, waits for them, and re-layouts  5.38 us (3%)
  loops' own time  3.75 us (2%)
    all_to_all x8, blocking collectives, exchange(): lax.all_to_all(blocks, axis, 0, 0, tiled=True, axis_index_groups=groups)  96.9 us
    ppermute x7, starting transfers between devices, around(): return lax.ppermute(value, 'section', pairs)  13.3 us
    all_to_all x2, starting transfers between devices, exchange(): lax.all_to_all(blocks, axis, 0, 0, tiled=True, axis_index_groups=groups)  10.5 us
    ppermute x7, waiting for transfers between devices, around(): return lax.ppermute(value, 'section', pairs)  9.06 us
    pallas_call x1, Pallas kernels, weight_gradients(): pl.pallas_call(kernel, compiler_params=grant(16), grid=(width // block,),...  7.35 us
    pallas_call x2, Pallas kernels, chain_step(): pl.pallas_call(kernel, compiler_params=grant(16), in_specs=[pl.BlockSpec(...  7.3 us
    pallas_call x1, Pallas kernels, first_pass(): pl.pallas_call(kernel, compiler_params=grant(28), in_specs=[smem] + [whol...  6.79 us
    ppermute x3, starting transfers between devices, from_partner(): return lax.ppermute(value, 'ep', [(i, i ^ 1) for i in range(devices)])  6.58 us
  transfers between devices with their start and end apart: 12, of which 7 were waited for; matrix products, arithmetic and copies ran while one was open for 0% of the time, Pallas kernels for 5%

profile of v1, /device:TPU:1, one launch (start us, length us, event | category | flops | bytes accessed | tf_op | source)
XLA Modules:
  0.0 184.9 jit_solution(3435524088392310078)
XLA Ops:
  3.2 2.5 %collective-permute-start.2 = (bf16[136,512]{1,0:T(8,128)(2,1)S(1)}, bf16[136,512]{1,0:T(8,128)(2,1)S(1)}, u32[]{:S(2)}, u32[]{:S(2)}) collective-permute-start(bf16[136,512]{1,0:T(8,128)(2,1)S(1)} %get-tuple-element.400.refs_0_), channel_id=1, source_target_pairs={{0,32},{32,64},{64,96},{96,128},{128,160},{160,192},{192,224},{224... | collective-permute-start | bytes 417800 | tf_op jit(solution)/shard_map/ppermute | solution.py:613
  5.7 1.2 copy-done
  6.9 1.1 shard_map.103
  8.0 6.9 %all-to-all-start.10 = ((bf16[16,8,2048]{2,1,0:T(8,128)(2,1)}), bf16[16,8,2048]{2,1,0:T(8,128)(2,1)S(1)}, u32[]{:S(2)}, u32[]{:S(2)}) async-start(bf16[16,8,2048]{2,1,0:T(8,128)(2,1)} %shard_map.103), calls=%async_computation.10 | async-start | bytes 1048576 | tf_op jit(solution)/shard_map/all_to_all | solution.py:19
  14.8 4.0 %collective-permute-start.3 = (bf16[136,512]{1,0:T(8,128)(2,1)S(1)}, bf16[136,512]{1,0:T(8,128)(2,1)S(1)}, u32[]{:S(2)}, u32[]{:S(2)}) collective-permute-start(bf16[136,512]{1,0:T(8,128)(2,1)S(1)} %get-tuple-element.400.refs_0_), channel_id=1, source_target_pairs={{0,224},{32,0},{64,32},{96,64},{128,96},{160,128},{192,160},{224,1... | collective-permute-start | bytes 417800 | tf_op jit(solution)/shard_map/ppermute | solution.py:613
  18.9 2.0 %collective-permute-done.3.refs_2_ = bf16[136,512]{1,0:T(8,128)(2,1)S(1)} collective-permute-done((bf16[136,512]{1,0:T(8,128)(2,1)S(1)}, bf16[136,512]{1,0:T(8,128)(2,1)S(1)}, u32[]{:S(2)}, u32[]{:S(2)}) %collective-permute-start.3) | collective-permute-done | bytes 139296 | tf_op jit(solution)/shard_map/ppermute | solution.py:613
  20.9 3.5 %collective-permute-start.5 = (bf16[136,512]{1,0:T(8,128)(2,1)S(1)}, bf16[136,512]{1,0:T(8,128)(2,1)S(1)}, u32[]{:S(2)}, u32[]{:S(2)}) collective-permute-start(bf16[136,512]{1,0:T(8,128)(2,1)S(1)} %collective-permute-done.3.refs_2_), channel_id=1, source_target_pairs={{0,224},{32,0},{64,32},{96,64},{128,96},{160,128},{192,160},{224,1... | collective-permute-start | bytes 417800 | tf_op jit(solution)/shard_map/ppermute | solution.py:613
  24.4 2.0 %collective-permute-done.5.refs_4_ = bf16[136,512]{1,0:T(8,128)(2,1)S(1)} collective-permute-done((bf16[136,512]{1,0:T(8,128)(2,1)S(1)}, bf16[136,512]{1,0:T(8,128)(2,1)S(1)}, u32[]{:S(2)}, u32[]{:S(2)}) %collective-permute-start.5) | collective-permute-done | bytes 139296 | tf_op jit(solution)/shard_map/ppermute | solution.py:613
  26.4 3.4 %collective-permute-start.7 = (bf16[136,512]{1,0:T(8,128)(2,1)S(1)}, bf16[136,512]{1,0:T(8,128)(2,1)S(1)}, u32[]{:S(2)}, u32[]{:S(2)}) collective-permute-start(bf16[136,512]{1,0:T(8,128)(2,1)S(1)} %collective-permute-done.5.refs_4_), channel_id=1, source_target_pairs={{0,224},{32,0},{64,32},{96,64},{128,96},{160,128},{192,160},{224,1... | collective-permute-start | bytes 417800 | tf_op jit(solution)/shard_map/ppermute | solution.py:613
  29.9 1.9 %collective-permute-done.7.refs_6_ = bf16[136,512]{1,0:T(8,128)(2,1)S(1)} collective-permute-done((bf16[136,512]{1,0:T(8,128)(2,1)S(1)}, bf16[136,512]{1,0:T(8,128)(2,1)S(1)}, u32[]{:S(2)}, u32[]{:S(2)}) %collective-permute-start.7) | collective-permute-done | bytes 139296 | tf_op jit(solution)/shard_map/ppermute | solution.py:613
  31.8 3.1 %collective-permute-done.8.refs_7_ = bf16[136,512]{1,0:T(8,128)(2,1)S(1)} collective-permute-done((bf16[136,512]{1,0:T(8,128)(2,1)S(1)}, bf16[136,512]{1,0:T(8,128)(2,1)S(1)}, u32[]{:S(2)}, u32[]{:S(2)}) %collective-permute-start.8) | collective-permute-done | bytes 139296 | tf_op jit(solution)/shard_map/ppermute | solution.py:613
  34.9 1.4 shard_map.104
  36.3 15.3 %all_to_all.67 = bf16[16,8,2176]{2,1,0:T(8,128)(2,1)S(1)} all-to-all(bf16[16,8,2176]{2,1,0:T(8,128)(2,1)S(1)} %get-tuple-element.410), channel_id=1, replica_groups={{0,2,4,6,8,10,12,14,16,18,20,22,24,26,28,30},{1,3,5,7,9,11,13,15,17,19,..., dimensions={0} | all-to-all | bytes 1114112 | tf_op jit(solution)/shard_map/all_to_all | solution.py:19
  51.6 6.1 %collective-permute-start.10 = (bf16[16,8,2176]{2,1,0:T(8,128)(2,1)S(1)}, bf16[16,8,2176]{2,1,0:T(8,128)(2,1)S(1)}, u32[]{:S(2)}, u32[]{:S(2)}) collective-permute-start(bf16[16,8,2176]{2,1,0:T(8,128)(2,1)S(1)} %all_to_all.67), channel_id=1, source_target_pairs={{0,1},{1,0},{2,3},{3,2},{4,5},{5,4},{6,7},{7,6},{8,9},{9,8},{10,11... | collective-permute-start | bytes 1671176 | tf_op jit(solution)/shard_map/ppermute | solution.py:27
  57.7 2.3 %collective-permute-done.9 = bf16[16,8,2048]{2,1,0:T(8,128)(2,1)S(1)} collective-permute-done((bf16[16,8,2048]{2,1,0:T(8,128)(2,1)S(1)}, bf16[16,8,2048]{2,1,0:T(8,128)(2,1)S(1)}, u32[]{:S(2)}, u32[]{:S(2)}) %collective-permute-start.9) | collective-permute-done | bytes 524320 | tf_op jit(solution)/shard_map/ppermute | solution.py:27
  60.1 6.8 %shard_map.105 = (bf16[16,128]{1,0:T(8,128)(2,1)}, bf16[16,256]{1,0:T(8,128)(2,1)}, f32[16,128]{1,0:T(8,128)S(1)}, f32[32,128]{1,0:T(8,128)S(1)}, bf16[256,128]{...) custom-call(s32[3]{0:T(128)} %copy-done.49, ...), custom_call_target="tpu_custom_call" | custom-call | tf_op jit(solution)/shard_map/pallas_call | solution.py:244
  67.5 116.4 %conditional.1 = (bf16[224,4096]{1,0:T(8,128)(2,1)}, bf16[224,4096]{1,0:T(8,128)(2,1)}, bf16[224,4096]{1,0:T(8,128)(2,1)}, bf16[1,128,4096]{2,1,0:T(8,128)(2,1)S(1)}) conditional(s32[]{:T(128)} %bitcast.40, (s32[]{:T(128)}, f32[32,128]{1,0:T(8,128)S(1)}, s32[]{:T(128)}, bf16[224,256]{1,0:T(8,128)(2,1)}, bf16[224,256]{1,0:T(8,128)(2,1)}, ...), branch_computations={%region_0.9_spmd, %region_9.14_spmd} | conditional | flops 703832320 | bytes 64377592 | solution.py:776
  68.6 82.2 %while.31 = (s32[]{:T(128)}, bf16[16,4096]{1,0:T(8,128)(2,1)}, bf16[224,16]{1,0:T(8,128)(2,1)}, bf16[224,16]{1,0:T(8,128)(2,1)}, bf16[32,16,128]{2,1,0:T(8,128)(...) while((s32[]{:T(128)}, bf16[16,4096]{1,0:T(8,128)(2,1)}, ...), condition=%wide.region_12.12_spmd, body=%wide.region_10.11_spmd.sunk | while | flops 153604 | bytes 901275 | solution.py:759
  69.9 11.2 %all_to_all.68 = bf16[32,16,128]{2,1,0:T(8,128)(2,1)S(1)} all-to-all(bf16[32,16,128]{2,1,0:T(8,128)(2,1)S(1)} %get-tuple-element.789), channel_id=1, replica_groups=mesh['section'=8,'ep'=32] {'ep'}, dimensions={0} | all-to-all | bytes 262144 | tf_op jit(solution)/shard_map/cond/branch_1_fun/while/body/all_to_all | solution.py:19
  81.2 12.6 %all_to_all.69.layers_ref = bf16[8,32,128]{2,1,0:T(8,128)(2,1)S(1)} all-to-all(bf16[8,32,128]{2,1,0:T(8,128)(2,1)S(1)} %broadcast_in_dim.96), channel_id=1, replica_groups=mesh['section'=8,'ep'=32] {'section'}, dimensions={0} | all-to-all | bytes 131072 | tf_op jit(solution)/shard_map/cond/branch_1_fun/while/body/all_to_all | solution.py:19
  94.7 12.7 %all_to_all.70.blocks_ref = bf16[32,16,128]{2,1,0:T(8,128)(2,1)S(1)} all-to-all(bf16[32,16,128]{2,1,0:T(8,128)(2,1)S(1)} %body.4), channel_id=1, replica_groups=mesh['section'=8,'ep'=32] {'ep'}, dimensions={0} | all-to-all | bytes 262144 | tf_op jit(solution)/shard_map/cond/branch_1_fun/while/body/all_to_all | solution.py:19
  107.3 4.5 %body.5 = (bf16[16,4096]{1,0:T(8,128)(2,1)}, bf16[224,16]{1,0:T(8,128)(2,1)}, bf16[224,16]{1,0:T(8,128)(2,1)}, bf16[32,16,128]{2,1,0:T(8,128)(2,1)S(1)}) custom-call(s32[1]{0:T(128)} %bitcast.86.last_ref, bf16[32,16,128]{2,1,0:T(8,128)(2,1)S(1)} %all_to_all.70.blocks_ref, f32[224,16]{1,0:T(8,128)S(1)} %get-tuple-element.858.act_ref, ...), custom_call_target="tpu_custom_call" | custom-call | tf_op jit(solution)/shard_map/cond/branch_1_fun/while/body/pallas_call | solution.py:329
  113.1 11.2 %all_to_all.68 = bf16[32,16,128]{2,1,0:T(8,128)(2,1)S(1)} all-to-all(bf16[32,16,128]{2,1,0:T(8,128)(2,1)S(1)} %get-tuple-element.789), channel_id=1, replica_groups=mesh['section'=8,'ep'=32] {'ep'}, dimensions={0} | all-to-all | bytes 262144 | tf_op jit(solution)/shard_map/cond/branch_1_fun/while/body/all_to_all | solution.py:19
  124.4 9.5 %all_to_all.69.layers_ref = bf16[8,32,128]{2,1,0:T(8,128)(2,1)S(1)} all-to-all(bf16[8,32,128]{2,1,0:T(8,128)(2,1)S(1)} %broadcast_in_dim.96), channel_id=1, replica_groups=mesh['section'=8,'ep'=32] {'section'}, dimensions={0} | all-to-all | bytes 131072 | tf_op jit(solution)/shard_map/cond/branch_1_fun/while/body/all_to_all | solution.py:19
  134.8 12.5 %all_to_all.70.blocks_ref = bf16[32,16,128]{2,1,0:T(8,128)(2,1)S(1)} all-to-all(bf16[32,16,128]{2,1,0:T(8,128)(2,1)S(1)} %body.4), channel_id=1, replica_groups=mesh['section'=8,'ep'=32] {'ep'}, dimensions={0} | all-to-all | bytes 262144 | tf_op jit(solution)/shard_map/cond/branch_1_fun/while/body/all_to_all | solution.py:19
  147.3 2.9 %body.5 = (bf16[16,4096]{1,0:T(8,128)(2,1)}, bf16[224,16]{1,0:T(8,128)(2,1)}, bf16[224,16]{1,0:T(8,128)(2,1)}, bf16[32,16,128]{2,1,0:T(8,128)(2,1)S(1)}) custom-call(s32[1]{0:T(128)} %bitcast.86.last_ref, bf16[32,16,128]{2,1,0:T(8,128)(2,1)S(1)} %all_to_all.70.blocks_ref, f32[224,16]{1,0:T(8,128)S(1)} %get-tuple-element.858.act_ref, ...), custom_call_target="tpu_custom_call" | custom-call | tf_op jit(solution)/shard_map/cond/branch_1_fun/while/body/pallas_call | solution.py:329
  150.8 3.2 %branch_1_fun.3 = (bf16[2,224,256]{2,1,0:T(8,128)(2,1)S(1)}, bf16[2,224,256]{2,1,0:T(8,128)(2,1)S(1)}, bf16[2,224,256]{2,1,0:T(8,128)(2,1)S(1)}, bf16[128,2048]{1,0:T(8,128)(2,1)S(1)}, bf16[128,2048]{1,0:T(8,128)(2,1)S(1)}) custom-call(bf16[16,256]{1,0:T(8,128)(2,1)} %get-tuple-element.303.pick_ref, bf16[224,256]{1,0:T(8,128)(2,1)} %get-tuple-element.304.gate_ref, ...), custom_call_target="tpu_custom_call" | custom-call | tf_op jit(solution)/shard_map/cond/branch_1_fun/pallas_call | solution.py:385
  154.6 1.5 collective-permute-done
  157.0 3.6 %all-to-all-start.3 = ((bf16[16,8,2048]{2,1,0:T(8,128)(2,1)}), bf16[16,8,2048]{2,1,0:T(8,128)(2,1)S(1)}, u32[]{:S(2)}, u32[]{:S(2)}) async-start(bf16[16,8,2048]{2,1,0:T(8,128)(2,1)} %fusion.5), calls=%async_computation.3 | async-start | bytes 1048576 | tf_op jit(solution)/shard_map/cond/branch_1_fun/all_to_all | solution.py:19
  160.7 7.4 %branch_1_fun.4 = (bf16[224,4096]{1,0:T(8,128)(2,1)}, bf16[224,4096]{1,0:T(8,128)(2,1)}, bf16[224,4096]{1,0:T(8,128)(2,1)}) custom-call(bf16[256,2048]{1,0:T(8,128)(2,1)S(1)} %copy-done.9, bf16[256,2048]{1,0:T(8,128)(2,1)} %get-tuple-element.325.y_ref, bf16[2,224,256]{2,1,0:T(8,128)(2,1)S(1)} %get-tuple-element.326.gate_ref, ...), custom_call_target="tpu_custom_call" | custom-call | tf_op jit(solution)/shard_map/cond/branch_1_fun/pallas_call | solution.py:410
  168.1 2.7 %all-to-all-done.3 = bf16[16,8,2048]{2,1,0:T(8,128)(2,1)S(1)} async-done(((bf16[16,8,2048]{2,1,0:T(8,128)(2,1)}), bf16[16,8,2048]{2,1,0:T(8,128)(2,1)S(1)}, u32[]{:S(2)}, u32[]{:S(2)}) %all-to-all-start.3) | async-done | bytes 524320 | tf_op jit(solution)/shard_map/cond/branch_1_fun/all_to_all | solution.py:19
  170.9 12.0 %all_to_all.66 = bf16[8,8,2048]{2,1,0:T(8,128)(2,1)S(1)} all-to-all(bf16[8,8,2048]{2,1,0:T(8,128)(2,1)S(1)} %broadcast_in_dim.72), channel_id=1, replica_groups=mesh['section'=8,'ep'=32] {'section'}, dimensions={0} | all-to-all | bytes 524288 | tf_op jit(solution)/shard_map/cond/branch_1_fun/all_to_all | solution.py:19
  (82 shorter events, 8.9 us)
Async XLA Ops:
  3.2 15.7 %collective-permute-start.2 = (bf16[136,512]{1,0:T(8,128)(2,1)S(1)}, bf16[136,512]{1,0:T(8,128)(2,1)S(1)}, u32[]{:S(2)}, u32[]{:S(2)}) collective-permute-start(bf16[136,512]{1,0:T(8,128)(2,1)S(1)} %get-tuple-element.400.refs_0_), channel_id=1, source_target_pairs={{0,32},{32,64},{64,96},{96,128},{128,160},{160,192},{192,224},{224... | collective-permute-start | bytes 417800 | tf_op jit(solution)/shard_map/ppermute | solution.py:613
  5.7 1.2 copy-start
  8.0 52.1 %copy-start.4 = (bf16[1,224,4096]{2,1,0:T(8,128)(2,1)S(1)}, bf16[1,224,4096]{2,1,0:T(8,128)(2,1)}, u32[]{:S(2)}) copy-start(bf16[1,224,4096]{2,1,0:T(8,128)(2,1)} %param.17) | copy-start | bytes 5505028
  8.0 23.8 %all-to-all-start.10 = ((bf16[16,8,2048]{2,1,0:T(8,128)(2,1)}), bf16[16,8,2048]{2,1,0:T(8,128)(2,1)S(1)}, u32[]{:S(2)}, u32[]{:S(2)}) async-start(bf16[16,8,2048]{2,1,0:T(8,128)(2,1)} %shard_map.103), calls=%async_computation.10 | async-start | bytes 1048576 | tf_op jit(solution)/shard_map/all_to_all | solution.py:19
  14.8 6.0 %collective-permute-start.3 = (bf16[136,512]{1,0:T(8,128)(2,1)S(1)}, bf16[136,512]{1,0:T(8,128)(2,1)S(1)}, u32[]{:S(2)}, u32[]{:S(2)}) collective-permute-start(bf16[136,512]{1,0:T(8,128)(2,1)S(1)} %get-tuple-element.400.refs_0_), channel_id=1, source_target_pairs={{0,224},{32,0},{64,32},{96,64},{128,96},{160,128},{192,160},{224,1... | collective-permute-start | bytes 417800 | tf_op jit(solution)/shard_map/ppermute | solution.py:613
  18.9 5.5 %collective-permute-start.4 = (bf16[136,512]{1,0:T(8,128)(2,1)S(1)}, bf16[136,512]{1,0:T(8,128)(2,1)S(1)}, u32[]{:S(2)}, u32[]{:S(2)}) collective-permute-start(bf16[136,512]{1,0:T(8,128)(2,1)S(1)} %collective-permute-done.2.refs_1_), channel_id=1, source_target_pairs={{0,32},{32,64},{64,96},{96,128},{128,160},{160,192},{192,224},{224... | collective-permute-start | bytes 417800 | tf_op jit(solution)/shard_map/ppermute | solution.py:613
  20.9 5.5 %collective-permute-start.5 = (bf16[136,512]{1,0:T(8,128)(2,1)S(1)}, bf16[136,512]{1,0:T(8,128)(2,1)S(1)}, u32[]{:S(2)}, u32[]{:S(2)}) collective-permute-start(bf16[136,512]{1,0:T(8,128)(2,1)S(1)} %collective-permute-done.3.refs_2_), channel_id=1, source_target_pairs={{0,224},{32,0},{64,32},{96,64},{128,96},{160,128},{192,160},{224,1... | collective-permute-start | bytes 417800 | tf_op jit(solution)/shard_map/ppermute | solution.py:613
  24.4 5.4 %collective-permute-start.6 = (bf16[136,512]{1,0:T(8,128)(2,1)S(1)}, bf16[136,512]{1,0:T(8,128)(2,1)S(1)}, u32[]{:S(2)}, u32[]{:S(2)}) collective-permute-start(bf16[136,512]{1,0:T(8,128)(2,1)S(1)} %collective-permute-done.4.refs_3_), channel_id=1, source_target_pairs={{0,32},{32,64},{64,96},{96,128},{128,160},{160,192},{192,224},{224... | collective-permute-start | bytes 417800 | tf_op jit(solution)/shard_map/ppermute | solution.py:613
  26.4 5.4 %collective-permute-start.7 = (bf16[136,512]{1,0:T(8,128)(2,1)S(1)}, bf16[136,512]{1,0:T(8,128)(2,1)S(1)}, u32[]{:S(2)}, u32[]{:S(2)}) collective-permute-start(bf16[136,512]{1,0:T(8,128)(2,1)S(1)} %collective-permute-done.5.refs_4_), channel_id=1, source_target_pairs={{0,224},{32,0},{64,32},{96,64},{128,96},{160,128},{192,160},{224,1... | collective-permute-start | bytes 417800 | tf_op jit(solution)/shard_map/ppermute | solution.py:613
  29.8 30.3 %copy-start.30 = (bf16[136,512]{1,0:T(8,128)(2,1)}, bf16[136,512]{1,0:T(8,128)(2,1)S(1)}, u32[]{:S(2)}) copy-start(bf16[136,512]{1,0:T(8,128)(2,1)S(1)} %collective-permute-done.6.refs_5_) | copy-start | bytes 417796
  29.8 5.1 %collective-permute-start.8 = (bf16[136,512]{1,0:T(8,128)(2,1)S(1)}, bf16[136,512]{1,0:T(8,128)(2,1)S(1)}, u32[]{:S(2)}, u32[]{:S(2)}) collective-permute-start(bf16[136,512]{1,0:T(8,128)(2,1)S(1)} %collective-permute-done.6.refs_5_), channel_id=1, source_target_pairs={{0,32},{32,64},{64,96},{96,128},{128,160},{160,192},{192,224},{224... | collective-permute-start | bytes 417800 | tf_op jit(solution)/shard_map/ppermute | solution.py:613
  29.9 30.2 %copy-start.49 = (s32[3]{0:T(128)}, s32[3]{0:T(128)S(1)}, u32[]{:S(2)}) copy-start(s32[3]{0:T(128)S(1)} %pad_add_fusion.where_ref) | copy-start | bytes 40
  31.8 28.2 %copy-start.33 = (bf16[136,512]{1,0:T(8,128)(2,1)}, bf16[136,512]{1,0:T(8,128)(2,1)S(1)}, u32[]{:S(2)}) copy-start(bf16[136,512]{1,0:T(8,128)(2,1)S(1)} %collective-permute-done.7.refs_6_) | copy-start | bytes 417796
  34.9 25.2 %copy-start.36 = (bf16[136,512]{1,0:T(8,128)(2,1)}, bf16[136,512]{1,0:T(8,128)(2,1)S(1)}, u32[]{:S(2)}) copy-start(bf16[136,512]{1,0:T(8,128)(2,1)S(1)} %collective-permute-done.8.refs_7_) | copy-start | bytes 417796
  51.6 8.4 %collective-permute-start.10 = (bf16[16,8,2176]{2,1,0:T(8,128)(2,1)S(1)}, bf16[16,8,2176]{2,1,0:T(8,128)(2,1)S(1)}, u32[]{:S(2)}, u32[]{:S(2)}) collective-permute-start(bf16[16,8,2176]{2,1,0:T(8,128)(2,1)S(1)} %all_to_all.67), channel_id=1, source_target_pairs={{0,1},{1,0},{2,3},{3,2},{4,5},{5,4},{6,7},{7,6},{8,9},{9,8},{10,11... | collective-permute-start | bytes 1671176 | tf_op jit(solution)/shard_map/ppermute | solution.py:27
  57.7 2.3 %collective-permute-start.9 = (bf16[16,8,2048]{2,1,0:T(8,128)(2,1)S(1)}, bf16[16,8,2048]{2,1,0:T(8,128)(2,1)S(1)}, u32[]{:S(2)}, u32[]{:S(2)}) collective-permute-start(bf16[16,8,2048]{2,1,0:T(8,128)(2,1)S(1)} %all-to-all-done.10), channel_id=1, source_target_pairs={{0,1},{1,0},{2,3},{3,2},{4,5},{5,4},{6,7},{7,6},{8,9},{9,8},{10,11... | collective-permute-start | bytes 1572872 | tf_op jit(solution)/shard_map/ppermute | solution.py:27
  67.8 83.0 %copy-start.41 = (bf16[224,256]{1,0:T(8,128)(2,1)S(1)}, bf16[224,256]{1,0:T(8,128)(2,1)}, u32[]{:S(2)}) copy-start(bf16[224,256]{1,0:T(8,128)(2,1)} %get-tuple-element.306.hidden_ref) | copy-start | bytes 344068 | tf_op jit(solution)/shard_map/cond
  154.1 6.5 %copy-start.9 = (bf16[256,2048]{1,0:T(8,128)(2,1)S(1)}, bf16[256,2048]{1,0:T(8,128)(2,1)}, u32[]{:S(2)}) copy-start(bf16[256,2048]{1,0:T(8,128)(2,1)} %get-tuple-element.324.x_ref) | copy-start | bytes 3145732 | tf_op jit(solution)/shard_map/cond
  154.1 6.5 %copy-start.46 = (bf16[224,16]{1,0:T(8,128)(2,1)S(1)}, bf16[224,16]{1,0:T(8,128)(2,1)}, u32[]{:S(2)}) copy-start(bf16[224,16]{1,0:T(8,128)(2,1)} %get-tuple-element.329.hf_ref) | copy-start | bytes 21508 | tf_op jit(solution)/shard_map/cond
  154.1 2.0 %collective-permute-start = (bf16[128,2048]{1,0:T(8,128)(2,1)S(1)}, bf16[128,2048]{1,0:T(8,128)(2,1)S(1)}, u32[]{:S(2)}, u32[]{:S(2)}) collective-permute-start(bf16[128,2048]{1,0:T(8,128)(2,1)S(1)} %get-tuple-element.323), channel_id=1, source_target_pairs={{0,1},{1,0},{2,3},{3,2},{4,5},{5,4},{6,7},{7,6},{8,9},{9,8},{10,11... | collective-permute-start | bytes 1572872 | tf_op jit(solution)/shard_map/cond/branch_1_fun/ppermute | solution.py:27
  157.0 13.7 %all-to-all-start.3 = ((bf16[16,8,2048]{2,1,0:T(8,128)(2,1)}), bf16[16,8,2048]{2,1,0:T(8,128)(2,1)S(1)}, u32[]{:S(2)}, u32[]{:S(2)}) async-start(bf16[16,8,2048]{2,1,0:T(8,128)(2,1)} %fusion.5), calls=%async_computation.3 | async-start | bytes 1048576 | tf_op jit(solution)/shard_map/cond/branch_1_fun/all_to_all | solution.py:19
  160.6 22.2 %copy-start.13 = (bf16[136,512]{1,0:T(8,128)(2,1)S(1)}, bf16[136,512]{1,0:T(8,128)(2,1)}, u32[]{:S(2)}) copy-start(bf16[136,512]{1,0:T(8,128)(2,1)} %copy-done.12) | copy-start | bytes 417796 | tf_op jit(solution)/shard_map/cond
  160.6 22.2 %copy-start.17 = (bf16[136,512]{1,0:T(8,128)(2,1)S(1)}, bf16[136,512]{1,0:T(8,128)(2,1)}, u32[]{:S(2)}) copy-start(bf16[136,512]{1,0:T(8,128)(2,1)} %copy-done.16) | copy-start | bytes 417796 | tf_op jit(solution)/shard_map/cond
  160.6 22.2 %copy-start.21 = (bf16[136,512]{1,0:T(8,128)(2,1)S(1)}, bf16[136,512]{1,0:T(8,128)(2,1)}, u32[]{:S(2)}) copy-start(bf16[136,512]{1,0:T(8,128)(2,1)} %copy-done.20) | copy-start | bytes 417796 | tf_op jit(solution)/shard_map/cond
  160.7 22.2 %copy-start.25 = (bf16[136,512]{1,0:T(8,128)(2,1)S(1)}, bf16[136,512]{1,0:T(8,128)(2,1)}, u32[]{:S(2)}) copy-start(bf16[136,512]{1,0:T(8,128)(2,1)} %copy-done.24) | copy-start | bytes 417796 | tf_op jit(solution)/shard_map/cond
  160.7 22.2 %copy-start.29 = (bf16[136,512]{1,0:T(8,128)(2,1)S(1)}, bf16[136,512]{1,0:T(8,128)(2,1)}, u32[]{:S(2)}) copy-start(bf16[136,512]{1,0:T(8,128)(2,1)} %copy-done.28) | copy-start | bytes 417796 | tf_op jit(solution)/shard_map/cond
  160.7 22.2 %copy-start.32 = (bf16[136,512]{1,0:T(8,128)(2,1)S(1)}, bf16[136,512]{1,0:T(8,128)(2,1)}, u32[]{:S(2)}) copy-start(bf16[136,512]{1,0:T(8,128)(2,1)} %get-tuple-element.344.refs_5_) | copy-start | bytes 417796 | tf_op jit(solution)/shard_map/cond
  160.7 22.2 %copy-start.35 = (bf16[136,512]{1,0:T(8,128)(2,1)S(1)}, bf16[136,512]{1,0:T(8,128)(2,1)}, u32[]{:S(2)}) copy-start(bf16[136,512]{1,0:T(8,128)(2,1)} %get-tuple-element.345.refs_6_) | copy-start | bytes 417796 | tf_op jit(solution)/shard_map/cond
  160.7 22.2 %copy-start.38 = (bf16[136,512]{1,0:T(8,128)(2,1)S(1)}, bf16[136,512]{1,0:T(8,128)(2,1)}, u32[]{:S(2)}) copy-start(bf16[136,512]{1,0:T(8,128)(2,1)} %get-tuple-element.346.refs_7_) | copy-start | bytes 417796 | tf_op jit(solution)/shard_map/cond
  160.7 22.2 %copy-start.48 = (f32[8,128]{1,0:T(8,128)S(1)}, f32[8,128]{1,0:T(8,128)}, u32[]{:S(2)}) copy-start(f32[8,128]{1,0:T(8,128)} %get-tuple-element.338.token_ref) | copy-start | bytes 12292 | tf_op jit(solution)/shard_map/cond
  160.7 22.2 %copy-start.51 = (s32[3]{0:T(128)S(1)}, s32[3]{0:T(128)}, u32[]{:S(2)}) copy-start(s32[3]{0:T(128)} %get-tuple-element.337.where_ref) | copy-start | bytes 40 | tf_op jit(solution)/shard_map/cond
  183.9 1.0 copy-start.39
  (8 other events, 6.0 us)
